TPU v7x, 32 devices: a whole 2x2x4 slice. The times are simulated.
32 devices in a mesh: grp: 4 (over y, x), zero: 8 (over z, core).
Axes of the slice: x: 2, y: 2, z: 4, core: 2. Of those that a mesh axis runs over, the one named last changes fastest.
Arguments:
- replica_grads: bfloat16 [4, 3072, 2, 12288], P('grp', None, None, 'zero'), may hold values from -20000 to 20000, as said below
- master_weights: float32 [3072, 2, 12288], P(('grp', 'zero')), may hold values from -0.6 to 0.6
- first_moment: float32 [3072, 2, 12288], P(('grp', 'zero')), may hold values from -0.3 to 0.3
- second_moment: float32 [3072, 2, 12288], P(('grp', 'zero')), may hold values from 0.001 to 0.03
- max_norm: float32 [1], replicated, may hold values from 1737.7856 to 4344.464
Outputs:
- new_master: float32 [3072, 2, 12288], P(('grp', 'zero'))
- new_first: float32 [3072, 2, 12288], P(('grp', 'zero'))
- new_second: float32 [3072, 2, 12288], P(('grp', 'zero'))
- new_weights: bfloat16 [3072, 2, 12288], P(None, None, 'zero')
Inputs may be any that keep to these rules, and one draw needn't show every extreme that they name: `replica_grads`: one gradient of the joined weight for each replica group.
All inputs are finite; a program needn't handle non-finite values.
Results may differ from a plain program's by a relative error of at most 0.015.
Values may be sent and summed in bfloat16 or wider, within the bound.
No kernel may reach another device: no remote copies, remote signals or barrier semaphores. Data moves between devices by JAX's collectives and lax.ppermute only.
A program may use at most 192 MiB of HBM per device.

v0:
```python
import jax
import jax.numpy as jnp
from jax import lax
from jax.sharding import PartitionSpec as P

ADAM_STEP = 10


beta_one = 0.9
beta_two = 0.95
learn_rate = 0.02
adam_eps = 1e-08
norm_eps = 1e-06


def adam_update(summed, master, first, second, scale):
    clipped = summed * scale
    new_first = beta_one * first + (1.0 - beta_one) * clipped
    new_second = beta_two * second + (1.0 - beta_two) * clipped * clipped
    correct_one = 1.0 - beta_one**ADAM_STEP
    correct_two = 1.0 - beta_two**ADAM_STEP
    step_size = new_first / correct_one / (jnp.sqrt(new_second / correct_two) + adam_eps)
    new_master = master - learn_rate * step_size
    return (new_master, new_first, new_second)


def body(replica_grads, master_weights, first_moment, second_moment, max_norm):
    groups = lax.axis_size("grp")
    shards = lax.axis_size("zero")
    local_grad = replica_grads[0]
    local_width = local_grad.shape[2]
    rows_dev = master_weights.shape[0]
    full_width = master_weights.shape[2]
    blocks = local_grad.reshape(groups, shards, rows_dev, 2, local_width)
    arrived = lax.all_to_all(
        lax.all_to_all(blocks[None], "grp", split_axis=1, concat_axis=0, tiled=True),
        "zero",
        split_axis=2,
        concat_axis=5,
        tiled=True,
    )
    summed = jnp.sum(arrived.astype(jnp.float32), axis=0)
    summed = summed.reshape(master_weights.shape)
    total = lax.psum(jnp.sum(summed * summed), ("grp", "zero"))
    scale = jnp.minimum(jnp.float32(1.0), max_norm[0] / (jnp.sqrt(total) + norm_eps))
    new_master, new_first, new_second = adam_update(
        summed, master_weights, first_moment, second_moment, scale
    )
    fresh = new_master.astype(jnp.bfloat16).reshape(1, 1, rows_dev, 2, full_width)
    own_tiles = lax.all_to_all(fresh, "zero", split_axis=4, concat_axis=1, tiled=True)
    tiled = lax.all_gather(own_tiles, "grp", axis=0, tiled=True)
    new_weights = tiled.reshape(groups * shards * rows_dev, 2, full_width // shards)
    return (new_master, new_first, new_second, new_weights)


def solution(mesh):
    in_specs = (
        P("grp", None, None, "zero"),
        P(("grp", "zero"), None, None),
        P(("grp", "zero"), None, None),
        P(("grp", "zero"), None, None),
        P(),
    )
    out_specs = (
        P(("grp", "zero"), None, None),
        P(("grp", "zero"), None, None),
        P(("grp", "zero"), None, None),
        P(None, None, "zero"),
    )
    return jax.shard_map(body, mesh=mesh, in_specs=in_specs, out_specs=out_specs, check_vma=False)
```

profile of v0, /device:TPU:0, one launch (start us, length us, event | category | flops | bytes accessed | tf_op | source)
XLA Modules:
  0.0 1264.3 jit_solution(17715620397299692491)
XLA Ops:
  7.2 0.0 all-gather.3.cloned.1.call-start
  7.2 218.8 %all_to_all.39 = bf16[1,4,8,96,2,1536]{5,4,3,2,0,1:T(2,128)(2,1)} all-to-all(bf16[1,4,8,96,2,1536]{5,4,3,2,0,1:T(2,128)(2,1)} %bitcast.20), channel_id=1, replica_groups=mesh['grp'=4,'zero'=8] {'grp'}, dimensions={1} | all-to-all | bytes 37748736 | tf_op jit(solution)/shard_map/all_to_all | solution.py:36
  226.0 15.4 %copy.48 = bf16[4,1,8,96,2,1536]{5,4,3,0,1,2:T(2,128)(2,1)S(1)} copy(bf16[4,1,8,96,2,1536]{5,4,3,2,0,1:T(2,128)(2,1)} %bitcast.16) | data formatting | bytes 37748736 | tf_op jit(solution)/shard_map/all_to_all | solution.py:36
  241.4 413.5 %all_to_all.40 = bf16[4,1,8,96,2,1536]{5,4,3,0,1,2:T(2,128)(2,1)} all-to-all(bf16[4,1,8,96,2,1536]{5,4,3,0,1,2:T(2,128)(2,1)S(1)} %copy.48), channel_id=1, replica_groups=mesh['grp'=4,'zero'=8] {'zero'}, dimensions={2} | all-to-all | bytes 37748736 | tf_op jit(solution)/shard_map/all_to_all | solution.py:35
  654.9 17.8 %convert_reduce_fusion = f32[8,96,2,1536]{3,1,2,0:T(8,128)} fusion(bf16[4,1,8,96,2,1536]{5,4,3,0,1,2:T(2,128)(2,1)} %all_to_all.40), kind=kLoop, calls=%fused_computation | loop fusion | flops 16515072 | bytes 28311552 | tf_op jit(solution)/shard_map/reduce_sum | solution.py:42
  672.7 14.0 %multiply_reduce_fusion = f32[]{:T(128)} fusion(f32[8,96,2,1536]{3,1,2,0:T(8,128)} %convert_reduce_fusion), kind=kLoop, calls=%fused_computation.8 | loop fusion | flops 4718591 | bytes 9437188 | tf_op jit(solution)/shard_map/reduce_sum | solution.py:44
  687.3 37.8 %psum.7 = f32[]{:T(128)} all-reduce(f32[]{:T(128)} %multiply_reduce_fusion), channel_id=1, replica_groups=mesh['grp'=4,'zero'=8] {'grp','zero'}, use_global_device_ids=true, to_apply=%region_2.0 | all-reduce | flops 1 | bytes 8 | tf_op jit(solution)/shard_map/psum | solution.py:44
  725.9 16.1 %multiply_bitcast_fusion = f32[96,2,8,1536]{3,1,0,2:T(2,128)S(1)} fusion(f32[8,96,2,1536]{3,1,2,0:T(8,128)} %convert_reduce_fusion, f32[]{:T(128)S(6)} %min_shard_map.3), kind=kLoop, calls=%fused_computation.7 | loop fusion | flops 2359296 | bytes 18874372 | tf_op jit(solution)/shard_map/mul | solution.py:17
  742.0 9.2 copy.51
  751.2 10.0 mul.56
  761.2 33.4 %convert_bitcast_fusion = (bf16[1,1,96,2,12288]{4,2,3,1,0:T(8,128)(2,1)}, f32[96,2,12288]{2,0,1:T(8,128)}, f32[96,2,12288]{2,0,1:T(8,128)}, f32[96,2,12288]{2,0,1:T(8,128)}) fusion(f32[96,2,12288]{2,1,0:T(2,128)} %param.6, f32[96,2,12288]{2,0,1:T(8,128)} %mul.56, f32[96,2,12288]{2,1,0:T(2,128)} %param.7, f32[96,2,12288]{2,1,0:T(2,128)} %param.8), kind=kLoop, calls=%fused_computation.9 | loop fusion | flops 33030144 | bytes 70778880 | tf_op jit(solution)/shard_map/reshape | solution.py:49
  794.7 14.1 %copy.54 = bf16[1,1,96,2,12288]{2,3,1,0,4:T(2,128)(2,1)} copy(bf16[1,1,96,2,12288]{4,2,3,1,0:T(8,128)(2,1)} %get-tuple-element.20) | data formatting | bytes 9437184 | tf_op jit(solution)/shard_map/reshape | solution.py:49
  808.7 144.7 %all_to_all.41 = bf16[1,1,96,2,12288]{2,3,1,0,4:T(2,128)(2,1)} all-to-all(bf16[1,1,96,2,12288]{2,3,1,0,4:T(2,128)(2,1)} %copy.54), channel_id=1, replica_groups=mesh['grp'=4,'zero'=8] {'zero'}, dimensions={4} | all-to-all | bytes 9437184 | tf_op jit(solution)/shard_map/all_to_all | solution.py:50
  953.5 15.8 %copy.55 = bf16[1,1,96,2,8,1536]{5,2,3,1,4,0:T(8,128)(2,1)} copy(bf16[1,1,96,2,8,1536]{2,3,5,4,1,0:T(2,128)(2,1)} %bitcast.19) | data formatting | bytes 9437184 | tf_op jit(solution)/shard_map/all_to_all | solution.py:50
  969.3 0.0 all-gather.3.cloned.1.call-update
  969.3 0.0 slice-start
  969.3 0.0 slice-start.1
  969.3 17.2 %copy.57 = f32[96,2,12288]{2,1,0:T(2,128)} copy(f32[96,2,12288]{2,0,1:T(8,128)} %get-tuple-element.21) | data formatting | bytes 18874368
  986.5 0.0 slice-start.2
  986.5 17.1 %copy.58 = f32[96,2,12288]{2,1,0:T(2,128)} copy(f32[96,2,12288]{2,0,1:T(8,128)} %get-tuple-element.22) | data formatting | bytes 18874368
  1003.7 0.0 slice-done
  1003.7 0.0 slice-done.1
  1003.7 0.0 slice-done.2
  1003.7 16.1 %copy.59 = f32[96,2,12288]{2,1,0:T(2,128)} copy(f32[96,2,12288]{2,0,1:T(8,128)S(1)} %bitcast.18) | data formatting | bytes 18874368
  1019.8 124.6 %all-gather.3.cloned.1.call-done = bf16[4,8,1,96,2,1536]{5,3,4,2,1,0:T(8,128)(2,1)} async-done(((bf16[1,8,1,96,2,1536]{5,3,4,2,1,0:T(8,128)(2,1)}), bf16[4,8,1,96,2,1536]{5,3,4,2,1,0:T(8,128)(2,1)}) %all-gather.3.cloned.1.call-update) | async-done | bytes 18874384 | tf_op jit(solution)/shard_map/all_gather | solution.py:51
  1144.3 9.5 copy.56
  1153.8 103.4 %copy.60 = bf16[3072,2,1536]{2,1,0:T(2,128)(2,1)} copy(bf16[3072,2,1536]{2,0,1:T(8,128)(2,1)S(1)} %bitcast.15) | data formatting | bytes 37748736
  (1 shorter events, 0.0 us)
Async XLA Ops:
  7.2 1137.2 %all-gather.3.cloned.1.call-start = ((), (), s32[]{:S(2)}) async-start(), calls=%async_computation.3 | async-start | bytes 23592960 | tf_op jit(solution)/shard_map/all_gather | solution.py:51
  969.3 34.4 %slice-start = ((s8[9437184]{0:T(1024)(128)(4,1)}), s8[4194304]{0:T(1024)(128)(4,1)S(1)}, s32[]{:S(2)}) async-start(s8[9437184]{0:T(1024)(128)(4,1)} %bitcast.17), calls=%async_computation.4 | async-start | bytes 8388608
  969.3 34.4 %slice-start.1 = ((s8[9437184]{0:T(1024)(128)(4,1)}), s8[4194304]{0:T(1024)(128)(4,1)S(1)}, s32[]{:S(2)}) async-start(s8[9437184]{0:T(1024)(128)(4,1)} %bitcast.17), calls=%async_computation.5 | async-start | bytes 8388608
  986.5 17.2 %slice-start.2 = ((s8[9437184]{0:T(1024)(128)(4,1)}), s8[1048576]{0:T(1024)(128)(4,1)S(1)}, s32[]{:S(2)}) async-start(s8[9437184]{0:T(1024)(128)(4,1)} %bitcast.17), calls=%async_computation.6 | async-start | bytes 2097152
Sparse Core Ops, SparseCore 0:
  969.4 174.8 all-gather.2
where the time goes:
time: 1270 us; the launch traced here: 1260 us
  blocking collectives  815 us (64%)
  local copies, waits for them, and re-layouts  228 us (18%)
  waiting for transfers between devices  125 us (10%)
  other arithmetic  81.3 us (6%)
  between operations  15.7 us (1%)
    all_to_all x1, blocking collectives, body(): lax.all_to_all(lax.all_to_all(blocks[None], 'grp', split_axis=1, concat_a...  414 us
    all_to_all x1, blocking collectives, body(): lax.all_to_all(blocks[None], 'grp', split_axis=1, concat_axis=0, tiled=True)  219 us
    unnamed x10, local copies, waits for them, and re-layouts  154 us
    all_to_all x1, blocking collectives, body(): lax.all_to_all(fresh, 'zero', split_axis=4, concat_axis=1, tiled=True)  145 us
    all_gather x1, waiting for transfers between devices, body(): tiled = lax.all_gather(own_tiles, 'grp', axis=0, tiled=True)  125 us
    psum x1, blocking collectives, body(): total = lax.psum(jnp.sum(summed * summed), ('grp', 'zero'))  37.8 us
    reshape x1, other arithmetic, body(): new_master.astype(jnp.bfloat16).reshape(1, 1, rows_dev, 2, full_width)  33.4 us
  transfers between devices with their start and end apart: 1, of which 1 were waited for; matrix products, arithmetic and copies ran while one was open for 4% of the time, Pallas kernels for 0%

commit v1 on v0

v1 whole, which is shorter than its diff:
```python
import functools

import jax
import jax.numpy as jnp
from jax import lax
from jax.experimental import pallas as pl
from jax.experimental.pallas import tpu as pltpu
from jax.sharding import PartitionSpec as P

ADAM_STEP = 10
LANES = 128
CHUNKS = 4

beta_one = 0.9
beta_two = 0.95
learn_rate = 0.02
adam_eps = 1e-08
norm_eps = 1e-06


def adam_update(summed, master, first, second, scale):
    clipped = summed * scale
    new_first = beta_one * first + (1.0 - beta_one) * clipped
    new_second = beta_two * second + (1.0 - beta_two) * clipped * clipped
    correct_one = 1.0 - beta_one**ADAM_STEP
    correct_two = 1.0 - beta_two**ADAM_STEP
    step_size = new_first / correct_one / (jnp.sqrt(new_second / correct_two) + adam_eps)
    new_master = master - learn_rate * step_size
    return (new_master, new_first, new_second)


def chunks_of(rows):
    return max(c for c in range(1, CHUNKS + 1) if rows % c == 0)


def to_blocks(x, blocks):
    rows, pair, columns = x.shape
    width = columns // blocks
    if width % LANES == 0:
        return x
    return x.reshape(rows, pair, blocks, width).transpose(0, 2, 1, 3)


def from_blocks(x):
    if x.ndim == 3:
        return x
    rows, blocks, pair, width = x.shape
    return x.transpose(0, 2, 1, 3).reshape(rows, pair, blocks * width)


def block_spec(x, rows, width, index):
    if x.ndim == 3:
        return pl.BlockSpec((rows, x.shape[1], width), lambda *at: (index(*at)[0], 0, index(*at)[1]))
    return pl.BlockSpec((rows, None, x.shape[2], width), lambda *at: index(*at) + (0, 0))


HBM = pl.BlockSpec(memory_space=pl.ANY)
SCALAR = pl.BlockSpec(memory_space=pltpu.SMEM)


def move_kernel(chunk, rows, steps, gather, at_ref, *refs):
    count = len(steps)
    if gather:
        whole, pieces = refs[0], refs[1 : 1 + count]
    else:
        pieces, whole = refs[:count], refs[-4]
    held, in_sems, out_sems = refs[-3:]
    ins, outs = [], []
    for slot in range(count):
        block = whole.at[at_ref[slot], :, pl.ds(chunk * rows, rows)]
        source, target = (block, pieces[slot]) if gather else (pieces[slot], block)
        ins.append(pltpu.make_async_copy(source, held.at[slot], in_sems.at[slot]))
        outs.append(pltpu.make_async_copy(held.at[slot], target, out_sems.at[slot]))
    for copy in ins:
        copy.start()
    for copy, out in zip(ins, outs):
        copy.wait()
        out.start()
    for out in outs:
        out.wait()


def move_scratch(count, shape):
    return [
        pltpu.VMEM((count,) + shape, jnp.bfloat16),
        pltpu.SemaphoreType.DMA((count,)),
        pltpu.SemaphoreType.DMA((count,)),
    ]


def take_pieces(whole, at, steps, chunk, rows):
    shape = (whole.shape[1], rows) + whole.shape[3:]
    piece = jax.ShapeDtypeStruct(shape, whole.dtype)
    return pl.pallas_call(
        functools.partial(move_kernel, chunk, rows, steps, True),
        in_specs=[SCALAR, HBM],
        out_specs=[HBM] * len(steps),
        out_shape=[piece] * len(steps),
        scratch_shapes=move_scratch(len(steps), shape),
        cost_estimate=pl.CostEstimate(flops=0, bytes_accessed=4 * len(steps) * piece.size, transcendentals=0),
    )(at, whole)


def put_pieces(whole, like, at, pieces, chunk):
    count, shape = len(pieces), pieces[0].shape
    before = [] if whole is None else [whole]
    return pl.pallas_call(
        functools.partial(move_kernel, chunk, shape[1], list(range(count)), False),
        in_specs=[SCALAR] + [HBM] * (count + len(before)),
        out_specs=HBM,
        out_shape=jax.ShapeDtypeStruct(like.shape, like.dtype),
        scratch_shapes=move_scratch(count, shape),
        input_output_aliases={count + 1: 0} if before else {},
        cost_estimate=pl.CostEstimate(flops=0, bytes_accessed=4 * count * pieces[0].size, transcendentals=0),
    )(at, *pieces, *before)


def sum_kernel(count, me_ref, own_ref, *refs):
    others, (sum_ref, square_ref) = refs[:count], refs[count:]
    total = own_ref[0, 0].astype(jnp.float32)
    for other in others:
        total = total + other[0].astype(jnp.float32)
    sum_ref[0] = total.astype(sum_ref.dtype)

    @pl.when(pl.program_id(0) == 0)
    def _():
        square_ref[...] = jnp.zeros_like(square_ref)

    square_ref[...] += jnp.sum(total * total, axis=0)


def sum_replicas(me, grads, others, chunk):
    shards, rows, pair, width = others[0].shape
    size = others[0].size
    piece = pl.BlockSpec((1, rows, pair, width), lambda z, me: (z, 0, 0, 0))
    return pl.pallas_call(
        functools.partial(sum_kernel, len(others)),
        grid_spec=pltpu.PrefetchScalarGridSpec(
            num_scalar_prefetch=1,
            grid=(shards,),
            in_specs=[pl.BlockSpec((1, 1, rows, pair, width), lambda z, me: (me[0], z, chunk, 0, 0))]
            + [piece] * len(others),
            out_specs=[piece, pl.BlockSpec((pair, width), lambda z, me: (0, 0))],
        ),
        out_shape=[
            jax.ShapeDtypeStruct(others[0].shape, jnp.bfloat16),
            jax.ShapeDtypeStruct((pair, width), jnp.float32),
        ],
        compiler_params=pltpu.CompilerParams(dimension_semantics=("arbitrary",)),
        cost_estimate=pl.CostEstimate(flops=6 * size, bytes_accessed=2 * size * (2 + len(others)), transcendentals=0),
    )(me, grads, *others)


def adam_kernel(scale_ref, sum_ref, *refs):
    states, (fresh_ref, *outs) = refs[:3], refs[-4:]
    new = adam_update(sum_ref[0].astype(jnp.float32), *(state[...] for state in states), scale_ref[0])
    for out_ref, value in zip(outs, new):
        out_ref[...] = value
    fresh_ref[0] = new[0].astype(fresh_ref.dtype)


def adam_chunk(scale, summed, states, before, chunk):
    shards, rows, pair, width = summed.shape
    size = summed.size
    piece = pl.BlockSpec((1, rows, pair, width), lambda z: (z, 0, 0, 0))
    state = block_spec(states[0], rows, width, lambda z: (chunk, z))
    return pl.pallas_call(
        adam_kernel,
        grid=(shards,),
        in_specs=[SCALAR, piece] + [state] * 3 + [HBM] * len(before),
        out_specs=[piece] + [state] * 3,
        out_shape=[jax.ShapeDtypeStruct(summed.shape, jnp.bfloat16)]
        + [jax.ShapeDtypeStruct(states[0].shape, jnp.float32)] * 3,
        input_output_aliases={5 + i: 1 + i for i in range(len(before))},
        compiler_params=pltpu.CompilerParams(dimension_semantics=("arbitrary",)),
        cost_estimate=pl.CostEstimate(flops=20 * size, bytes_accessed=28 * size, transcendentals=2 * size),
    )(scale, summed, *states, *before)


def body(replica_grads, master_weights, first_moment, second_moment, max_norm):
    groups = lax.axis_size("grp")
    shards = lax.axis_size("zero")
    me = lax.axis_index("grp")
    pair = master_weights.shape[1]
    rows_dev = master_weights.shape[0]
    chunks = chunks_of(rows_dev)
    rows = rows_dev // chunks

    width = replica_grads.shape[3]
    grads = replica_grads.reshape(groups, shards, rows_dev, pair, width)
    states = [to_blocks(x, shards) for x in (master_weights, first_moment, second_moment)]

    def swap(x, step):
        return lax.ppermute(x, "grp", [(i, i ^ step) for i in range(groups)])

    def spread(x):
        return lax.all_to_all(x, "zero", split_axis=0, concat_axis=0, tiled=True)

    steps = list(range(1, groups))
    at = jnp.stack([me ^ step for step in range(groups)])

    sums, squares = [], []
    for c in range(chunks):
        pieces = take_pieces(grads, at[1:], steps, c, rows)
        others = []
        for step, piece in zip(steps, pieces):
            others.append(swap(piece, step))
        summed, square = sum_replicas(me.reshape(1), grads, others, c)
        squares.append(square)
        sums.append(spread(summed))

    partial = jnp.sum(sum(squares[1:], squares[0]))
    parts = lax.all_to_all(
        jnp.broadcast_to(partial, (groups * shards, LANES)), ("grp", "zero"), split_axis=0, concat_axis=0, tiled=True
    )
    total = jnp.sum(parts[:, 0])
    scale = jnp.minimum(jnp.float32(1.0), max_norm / (jnp.sqrt(total) + norm_eps))

    outs, weights = [], None
    for c in range(chunks):
        fresh, *outs = adam_chunk(scale, sums[c], states, outs, c)
        blocks = {0: spread(fresh)}
        for far in range(1, groups):
            low = far & -far
            high = far ^ low
            before, last = (0, far) if high == 0 else ((low, high) if c % 2 == 0 else (high, low))
            blocks[far] = swap(blocks[before], last)
        near = [step for step in blocks if step == 0 or step & (step - 1) == 0]
        for group in (near, [step for step in blocks if step not in near]):
            weights = put_pieces(
                weights, grads, jnp.stack([me ^ step for step in group]), [blocks[step] for step in group], c
            )

    return tuple(from_blocks(x) for x in outs) + (weights.reshape(replica_grads.shape[1:]),)


def solution(mesh):
    in_specs = (
        P("grp", None, None, "zero"),
        P(("grp", "zero"), None, None),
        P(("grp", "zero"), None, None),
        P(("grp", "zero"), None, None),
        P(),
    )
    out_specs = (
        P(("grp", "zero"), None, None),
        P(("grp", "zero"), None, None),
        P(("grp", "zero"), None, None),
        P(None, None, "zero"),
    )

    return jax.shard_map(body, mesh=mesh, in_specs=in_specs, out_specs=out_specs, check_vma=False)
```

time: 1270 us -> 638 us (0.50)
  blocking collectives: 815 us -> 111 us
  waiting for transfers between devices: 125 us -> 357 us
  local copies, waits for them, and re-layouts: 228 us -> 6.18 us
  Pallas kernels: 0 us -> 106 us
  other arithmetic: 81.3 us -> 3.17 us
  starting transfers between devices: 0.04 us -> 50.4 us
  between operations: 15.7 us -> 2.29 us
    all_to_all x3 -> x4, blocking collectives: 777 us -> 111 us  [the longest x3 98.8 us: spread(): return lax.all_to_all(x, 'zero', split_axis=0, concat_axis=0, tiled=True)]
    ppermute x0 -> x24, waiting for transfers between devices: none -> 256 us  [swap(): return lax.ppermute(x, 'grp', [(i, i ^ step) for i in range(groups)])]
    unnamed x10 -> x30, local copies, waits for them, and re-layouts: 154 us -> 5.53 us
    all_gather x1 -> x0, waiting for transfers between devices: 125 us -> none  [body(): tiled = lax.all_gather(own_tiles, 'grp', axis=0, tiled=True)]
    pallas_call x0 -> x20, Pallas kernels: none -> 106 us  [the longest x4 39.2 us: adam_chunk(): pl.pallas_call(adam_kernel, grid=(shards,), in_specs=[SCALAR, piece] + [s...]
    all_to_all x0 -> x5, waiting for transfers between devices: none -> 101 us  [spread(): return lax.all_to_all(x, 'zero', split_axis=0, concat_axis=0, tiled=True)]
    psum x1 -> x0, blocking collectives: 37.8 us -> none  [body(): total = lax.psum(jnp.sum(summed * summed), ('grp', 'zero'))]
    reshape x1 -> x0, other arithmetic: 33.4 us -> none  [body(): new_master.astype(jnp.bfloat16).reshape(1, 1, rows_dev, 2, full_width)]
  transfers between devices with their start and end apart: 1 -> 29, of which waited for: 1 -> 17; matrix products, arithmetic and copies ran while one was open for 4% -> 0% of each run, Pallas kernels for 0% -> 15%
where the time goes in v1:
time: 638 us; the launch traced here: 636 us
  waiting for transfers between devices  357 us (56%)
  blocking collectives  111 us (17%)
  Pallas kernels  106 us (17%)
  starting transfers between devices  50.4 us (8%)
    ppermute x24, waiting for transfers between devices, swap(): return lax.ppermute(x, 'grp', [(i, i ^ step) for i in range(groups)])  256 us
    all_to_all x5, waiting for transfers between devices, spread(): return lax.all_to_all(x, 'zero', split_axis=0, concat_axis=0, tiled=True)  101 us
    all_to_all x3, blocking collectives, spread(): return lax.all_to_all(x, 'zero', split_axis=0, concat_axis=0, tiled=True)  98.8 us
    pallas_call x4, Pallas kernels, adam_chunk(): pl.pallas_call(adam_kernel, grid=(shards,), in_specs=[SCALAR, piece] + [s...  39.2 us
    ppermute x24, starting transfers between devices, swap(): return lax.ppermute(x, 'grp', [(i, i ^ step) for i in range(groups)])  31.9 us
    pallas_call x4, Pallas kernels, sum_replicas(): pl.pallas_call(functools.partial(sum_kernel, len(others)), grid_spec=pltp...  27.7 us
    pallas_call x8, Pallas kernels, put_pieces(): pl.pallas_call(functools.partial(move_kernel, chunk, shape[1], list(range...  24.3 us
    all_to_all x5, starting transfers between devices, spread(): return lax.all_to_all(x, 'zero', split_axis=0, concat_axis=0, tiled=True)  18.5 us
  transfers between devices with their start and end apart: 29, of which 17 were waited for; matrix products, arithmetic and copies ran while one was open for 0% of the time, Pallas kernels for 15%

profile of v1, /device:TPU:0, one launch (start us, length us, event | category | flops | bytes accessed | tf_op | source)
XLA Modules:
  0.0 636.1 jit_solution(6768951674958815946)
XLA Ops:
  1.2 3.8 shard_map.84
  5.0 3.0 collective-permute-start
  9.6 3.7 shard_map.86
  16.9 3.8 shard_map.88
  20.7 14.4 %collective-permute-done.refs_0_ = bf16[8,24,2,1536]{3,2,1,0:T(2,128)(2,1)S(1)} collective-permute-done((bf16[8,24,2,1536]{3,2,1,0:T(2,128)(2,1)}, bf16[8,24,2,1536]{3,2,1,0:T(2,128)(2,1)S(1)}, u32[]{:S(2)}, u32[]{:S(2)}) %collective-permute-start) | collective-permute-done | bytes 1179680 | tf_op jit(solution)/shard_map/ppermute | solution.py:194
  35.1 3.0 collective-permute-start.5
  38.1 24.3 %collective-permute-done.1.refs_1_ = bf16[8,24,2,1536]{3,2,1,0:T(2,128)(2,1)S(1)} collective-permute-done((bf16[8,24,2,1536]{3,2,1,0:T(2,128)(2,1)}, bf16[8,24,2,1536]{3,2,1,0:T(2,128)(2,1)S(1)}, u32[]{:S(2)}, u32[]{:S(2)}) %collective-permute-start.1) | collective-permute-done | bytes 1179680 | tf_op jit(solution)/shard_map/ppermute | solution.py:194
  64.4 21.3 %collective-permute-done.3.refs_0_ = bf16[8,24,2,1536]{3,2,1,0:T(2,128)(2,1)} collective-permute-done((bf16[8,24,2,1536]{3,2,1,0:T(2,128)(2,1)}, bf16[8,24,2,1536]{3,2,1,0:T(2,128)(2,1)}, u32[]{:S(2)}, u32[]{:S(2)}) %collective-permute-start.3) | collective-permute-done | bytes 1179680 | tf_op jit(solution)/shard_map/ppermute | solution.py:194
  85.8 3.0 collective-permute-start.8
  88.8 3.8 shard_map.90
  92.6 20.5 %collective-permute-done.4.refs_1_ = bf16[8,24,2,1536]{3,2,1,0:T(2,128)(2,1)} collective-permute-done((bf16[8,24,2,1536]{3,2,1,0:T(2,128)(2,1)}, bf16[8,24,2,1536]{3,2,1,0:T(2,128)(2,1)}, u32[]{:S(2)}, u32[]{:S(2)}) %collective-permute-start.4) | collective-permute-done | bytes 1179680 | tf_op jit(solution)/shard_map/ppermute | solution.py:194
  114.6 21.8 %collective-permute-done.6.refs_0_ = bf16[8,24,2,1536]{3,2,1,0:T(2,128)(2,1)} collective-permute-done((bf16[8,24,2,1536]{3,2,1,0:T(2,128)(2,1)}, bf16[8,24,2,1536]{3,2,1,0:T(2,128)(2,1)}, u32[]{:S(2)}, u32[]{:S(2)}) %collective-permute-start.6) | collective-permute-done | bytes 1179680 | tf_op jit(solution)/shard_map/ppermute | solution.py:194
  138.4 6.9 %shard_map.85 = (bf16[8,24,2,1536]{3,2,1,0:T(2,128)(2,1)}, f32[2,1536]{1,0:T(2,128)}) custom-call(s32[1]{0:T(128)} %bitcast.me_ref, bf16[4,8,96,2,1536]{4,3,2,1,0:T(2,128)(2,1)} %bitcast.13, bf16[8,24,2,1536]{3,2,1,0:T(2,128)(2,1)} %copy-done.4, bf16[8,24,2,1536]{3,2,1,0:T(2,128)(2,1)} %copy-done.5, bf16[8,24,2,1536]{3,2,1,0:T(2,128)(2,1)} %copy-done.6), custom_call_target="tpu_custom_call" | custom-call | flops 3538944 | bytes 5898240 | tf_op jit(solution)/shard_map/pallas_call | solution.py:136
  145.3 6.9 %shard_map.87 = (bf16[8,24,2,1536]{3,2,1,0:T(2,128)(2,1)}, f32[2,1536]{1,0:T(2,128)}) custom-call(s32[1]{0:T(128)} %bitcast.me_ref, bf16[4,8,96,2,1536]{4,3,2,1,0:T(2,128)(2,1)} %bitcast.14, bf16[8,24,2,1536]{3,2,1,0:T(2,128)(2,1)} %collective-permute-done.3.refs_0_, bf16[8,24,2,1536]{3,2,1,0:T(2,128)(2,1)} %collective-permute-done.4.refs_1_, ...), custom_call_target="tpu_custom_call" | custom-call | flops 3538944 | bytes 5898240 | tf_op jit(solution)/shard_map/pallas_call | solution.py:136
  152.3 36.6 %collective-permute-done.7.refs_1_ = bf16[8,24,2,1536]{3,2,1,0:T(2,128)(2,1)} collective-permute-done((bf16[8,24,2,1536]{3,2,1,0:T(2,128)(2,1)}, bf16[8,24,2,1536]{3,2,1,0:T(2,128)(2,1)}, u32[]{:S(2)}, u32[]{:S(2)}) %collective-permute-start.7) | collective-permute-done | bytes 1179680 | tf_op jit(solution)/shard_map/ppermute | solution.py:194
  188.9 6.9 %shard_map.89 = (bf16[8,24,2,1536]{3,2,1,0:T(2,128)(2,1)}, f32[2,1536]{1,0:T(2,128)}) custom-call(s32[1]{0:T(128)} %bitcast.me_ref, bf16[4,8,96,2,1536]{4,3,2,1,0:T(2,128)(2,1)} %bitcast.15, bf16[8,24,2,1536]{3,2,1,0:T(2,128)(2,1)} %collective-permute-done.6.refs_0_, bf16[8,24,2,1536]{3,2,1,0:T(2,128)(2,1)} %collective-permute-done.7.refs_1_, ...), custom_call_target="tpu_custom_call" | custom-call | flops 3538944 | bytes 5898240 | tf_op jit(solution)/shard_map/pallas_call | solution.py:136
  195.8 16.8 %collective-permute-done.10.refs_1_ = bf16[8,24,2,1536]{3,2,1,0:T(2,128)(2,1)S(1)} collective-permute-done((bf16[8,24,2,1536]{3,2,1,0:T(2,128)(2,1)}, bf16[8,24,2,1536]{3,2,1,0:T(2,128)(2,1)S(1)}, u32[]{:S(2)}, u32[]{:S(2)}) %collective-permute-start.10) | collective-permute-done | bytes 1179680 | tf_op jit(solution)/shard_map/ppermute | solution.py:194
  215.1 6.9 %shard_map.91 = (bf16[8,24,2,1536]{3,2,1,0:T(2,128)(2,1)}, f32[2,1536]{1,0:T(2,128)}) custom-call(s32[1]{0:T(128)} %bitcast.me_ref, bf16[4,8,96,2,1536]{4,3,2,1,0:T(2,128)(2,1)} %bitcast.16, bf16[8,24,2,1536]{3,2,1,0:T(2,128)(2,1)} %copy-done.11, bf16[8,24,2,1536]{3,2,1,0:T(2,128)(2,1)} %copy-done.7, bf16[8,24,2,1536]{3,2,1,0:T(2,128)(2,1)} %copy-done.8), custom_call_target="tpu_custom_call" | custom-call | flops 3538944 | bytes 5898240 | tf_op jit(solution)/shard_map/pallas_call | solution.py:136
  224.0 11.9 %all_to_all.49 = f32[32,1,128]{2,1,0:T(1,128)S(1)} all-to-all(f32[32,1,128]{2,1,0:T(1,128)S(1)} %broadcast_in_dim.3), channel_id=1, replica_groups=mesh['grp'=4,'zero'=8] {'grp','zero'}, dimensions={0} | all-to-all | bytes 32768 | tf_op jit(solution)/shard_map/all_to_all | solution.py:213
  235.9 33.8 %all_to_all.50.sum_ref = bf16[8,24,2,1536]{3,2,1,0:T(2,128)(2,1)} all-to-all(bf16[8,24,2,1536]{3,2,1,0:T(2,128)(2,1)} %get-tuple-element.59), channel_id=1, replica_groups=mesh['grp'=4,'zero'=8] {'zero'}, dimensions={0} | all-to-all | bytes 2359296 | tf_op jit(solution)/shard_map/all_to_all | solution.py:197
  269.7 32.6 %all_to_all.51.sum_ref = bf16[8,24,2,1536]{3,2,1,0:T(2,128)(2,1)} all-to-all(bf16[8,24,2,1536]{3,2,1,0:T(2,128)(2,1)S(1)} %copy-done.12), channel_id=1, replica_groups=mesh['grp'=4,'zero'=8] {'zero'}, dimensions={0} | all-to-all | bytes 2359296 | tf_op jit(solution)/shard_map/all_to_all | solution.py:197
  302.3 32.5 %all_to_all.52.sum_ref = bf16[8,24,2,1536]{3,2,1,0:T(2,128)(2,1)} all-to-all(bf16[8,24,2,1536]{3,2,1,0:T(2,128)(2,1)S(1)} %copy-done.13), channel_id=1, replica_groups=mesh['grp'=4,'zero'=8] {'zero'}, dimensions={0} | all-to-all | bytes 2359296 | tf_op jit(solution)/shard_map/all_to_all | solution.py:197
  334.8 3.6 all-to-all-start.1
  340.3 9.8 %shard_map.92 = (bf16[8,24,2,1536]{3,2,1,0:T(2,128)(2,1)}, f32[96,2,12288]{2,1,0:T(2,128)}, f32[96,2,12288]{2,1,0:T(2,128)}, f32[96,2,12288]{2,1,0:T(2,128)}) custom-call(f32[1]{0:T(128)S(6)} %min.3.scale_ref, bf16[8,24,2,1536]{3,2,1,0:T(2,128)(2,1)} %all_to_all.50.sum_ref, f32[96,2,12288]{2,1,0:T(2,128)} %refs_0_.7, f32[96,2,12288]{2,1,0:T(2,128)} %refs_1_.7, ...), custom_call_target="tpu_custom_call" | custom-call | flops 11796480 | bytes 16515072 | tf_op jit(solution)/shard_map/pallas_call | solution.py:167
  350.1 17.5 %all-to-all-done.1.sum_ref = bf16[8,24,2,1536]{3,2,1,0:T(2,128)(2,1)S(1)} async-done(((bf16[8,24,2,1536]{3,2,1,0:T(2,128)(2,1)}), bf16[8,24,2,1536]{3,2,1,0:T(2,128)(2,1)S(1)}, u32[]{:S(2)}, u32[]{:S(2)}) %all-to-all-start.1) | async-done | bytes 1179680 | tf_op jit(solution)/shard_map/all_to_all | solution.py:197
  368.7 3.6 all-to-all-start.8
  372.2 9.8 %shard_map.93 = (bf16[8,24,2,1536]{3,2,1,0:T(2,128)(2,1)}, f32[96,2,12288]{2,1,0:T(2,128)}, f32[96,2,12288]{2,1,0:T(2,128)}, f32[96,2,12288]{2,1,0:T(2,128)}) custom-call(f32[1]{0:T(128)S(6)} %min.3.scale_ref, bf16[8,24,2,1536]{3,2,1,0:T(2,128)(2,1)} %all_to_all.51.sum_ref, ...), custom_call_target="tpu_custom_call", output_to_operand_aliasing={{1}: (5, {}), {2}: (6, {}), {3}: (7, {})} | custom-call | flops 11796480 | bytes 16515072 | tf_op jit(solution)/shard_map/pallas_call | solution.py:167
  382.0 19.5 %all-to-all-done.8.refs_0_ = bf16[8,24,2,1536]{3,2,1,0:T(2,128)(2,1)S(1)} async-done(((bf16[8,24,2,1536]{3,2,1,0:T(2,128)(2,1)}), bf16[8,24,2,1536]{3,2,1,0:T(2,128)(2,1)S(1)}, u32[]{:S(2)}, u32[]{:S(2)}) %all-to-all-start.8) | async-done | bytes 1179680 | tf_op jit(solution)/shard_map/all_to_all | solution.py:197
  401.5 3.6 all-to-all-start.7
  405.1 9.8 %shard_map.94 = (bf16[8,24,2,1536]{3,2,1,0:T(2,128)(2,1)}, f32[96,2,12288]{2,1,0:T(2,128)}, f32[96,2,12288]{2,1,0:T(2,128)}, f32[96,2,12288]{2,1,0:T(2,128)}) custom-call(f32[1]{0:T(128)S(6)} %min.3.scale_ref, bf16[8,24,2,1536]{3,2,1,0:T(2,128)(2,1)} %all_to_all.52.sum_ref, ...), custom_call_target="tpu_custom_call", output_to_operand_aliasing={{1}: (5, {}), {2}: (6, {}), {3}: (7, {})} | custom-call | flops 11796480 | bytes 16515072 | tf_op jit(solution)/shard_map/pallas_call | solution.py:167
  414.9 19.5 %all-to-all-done.7.refs_0_ = bf16[8,24,2,1536]{3,2,1,0:T(2,128)(2,1)S(1)} async-done(((bf16[8,24,2,1536]{3,2,1,0:T(2,128)(2,1)}), bf16[8,24,2,1536]{3,2,1,0:T(2,128)(2,1)S(1)}, u32[]{:S(2)}, u32[]{:S(2)}) %all-to-all-start.7) | async-done | bytes 1179680 | tf_op jit(solution)/shard_map/all_to_all | solution.py:197
  434.4 3.6 all-to-all-start.6
  438.0 9.8 %shard_map.95 = (bf16[8,24,2,1536]{3,2,1,0:T(2,128)(2,1)}, f32[96,2,12288]{2,1,0:T(2,128)}, f32[96,2,12288]{2,1,0:T(2,128)}, f32[96,2,12288]{2,1,0:T(2,128)}) custom-call(f32[1]{0:T(128)S(6)} %min.3.scale_ref, bf16[8,24,2,1536]{3,2,1,0:T(2,128)(2,1)} %copy-done.3, ...), custom_call_target="tpu_custom_call", output_to_operand_aliasing={{1}: (5, {}), {2}: (6, {}), {3}: (7, {})} | custom-call | flops 11796480 | bytes 16515072 | tf_op jit(solution)/shard_map/pallas_call | solution.py:167
  447.7 19.5 %all-to-all-done.6.refs_0_ = bf16[8,24,2,1536]{3,2,1,0:T(2,128)(2,1)S(1)} async-done(((bf16[8,24,2,1536]{3,2,1,0:T(2,128)(2,1)}), bf16[8,24,2,1536]{3,2,1,0:T(2,128)(2,1)S(1)}, u32[]{:S(2)}, u32[]{:S(2)}) %all-to-all-start.6) | async-done | bytes 1179680 | tf_op jit(solution)/shard_map/all_to_all | solution.py:197
  467.3 4.3 all-to-all-start.5
  476.2 24.7 %all-to-all-done.5.refs_0_ = bf16[8,24,2,1536]{3,2,1,0:T(2,128)(2,1)} async-done(((bf16[8,24,2,1536]{3,2,1,0:T(2,128)(2,1)}), bf16[8,24,2,1536]{3,2,1,0:T(2,128)(2,1)}, u32[]{:S(2)}, u32[]{:S(2)}) %all-to-all-start.5) | async-done | bytes 1179680 | tf_op jit(solution)/shard_map/all_to_all | solution.py:197
  502.9 23.5 %collective-permute-done.18.refs_2_ = bf16[8,24,2,1536]{3,2,1,0:T(2,128)(2,1)} collective-permute-done((bf16[8,24,2,1536]{3,2,1,0:T(2,128)(2,1)S(1)}, bf16[8,24,2,1536]{3,2,1,0:T(2,128)(2,1)}, u32[]{:S(2)}, u32[]{:S(2)}) %collective-permute-start.18) | collective-permute-done | bytes 1179680 | tf_op jit(solution)/shard_map/ppermute | solution.py:194
  528.5 22.6 %collective-permute-done.15.refs_1_ = bf16[8,24,2,1536]{3,2,1,0:T(2,128)(2,1)} collective-permute-done((bf16[8,24,2,1536]{3,2,1,0:T(2,128)(2,1)S(1)}, bf16[8,24,2,1536]{3,2,1,0:T(2,128)(2,1)}, u32[]{:S(2)}, u32[]{:S(2)}) %collective-permute-start.15) | collective-permute-done | bytes 1179680 | tf_op jit(solution)/shard_map/ppermute | solution.py:194
  553.1 23.8 %collective-permute-done.22.refs_0_ = bf16[8,24,2,1536]{3,2,1,0:T(2,128)(2,1)} collective-permute-done((bf16[8,24,2,1536]{3,2,1,0:T(2,128)(2,1)}, bf16[8,24,2,1536]{3,2,1,0:T(2,128)(2,1)}, u32[]{:S(2)}, u32[]{:S(2)}) %collective-permute-start.22) | collective-permute-done | bytes 1179680 | tf_op jit(solution)/shard_map/ppermute | solution.py:194
  579.0 3.8 shard_map.96.refs_1_
  582.8 2.3 shard_map.97.refs_3_
  585.1 3.8 shard_map.98.refs_1_
  588.9 2.3 shard_map.99.refs_3_
  591.2 10.9 %collective-permute-done.17.refs_2_ = bf16[8,24,2,1536]{3,2,1,0:T(2,128)(2,1)S(1)} collective-permute-done((bf16[8,24,2,1536]{3,2,1,0:T(2,128)(2,1)S(1)}, bf16[8,24,2,1536]{3,2,1,0:T(2,128)(2,1)S(1)}, u32[]{:S(2)}, u32[]{:S(2)}) %collective-permute-start.17) | collective-permute-done | bytes 1179680 | tf_op jit(solution)/shard_map/ppermute | solution.py:194
  603.2 3.8 shard_map.100.refs_1_
  606.9 19.7 %collective-permute-done.16.refs_0_ = bf16[8,24,2,1536]{3,2,1,0:T(2,128)(2,1)} collective-permute-done((bf16[8,24,2,1536]{3,2,1,0:T(2,128)(2,1)}, bf16[8,24,2,1536]{3,2,1,0:T(2,128)(2,1)}, u32[]{:S(2)}, u32[]{:S(2)}) %collective-permute-start.16) | collective-permute-done | bytes 1179680 | tf_op jit(solution)/shard_map/ppermute | solution.py:194
  626.6 2.3 shard_map.101.refs_3_
  628.9 3.8 shard_map.102.refs_1_
  (69 shorter events, 34.6 us)
Async XLA Ops:
  5.0 30.1 %collective-permute-start = (bf16[8,24,2,1536]{3,2,1,0:T(2,128)(2,1)}, bf16[8,24,2,1536]{3,2,1,0:T(2,128)(2,1)S(1)}, u32[]{:S(2)}, u32[]{:S(2)}) collective-permute-start(bf16[8,24,2,1536]{3,2,1,0:T(2,128)(2,1)} %get-tuple-element.40), channel_id=1, source_target_pairs={{0,8},{8,0},{16,24},{24,16},{1,9},{9,1},{17,25},{25,17},{2,10},{10... | collective-permute-start | bytes 3538952 | tf_op jit(solution)/shard_map/ppermute | solution.py:194
  8.1 54.3 %collective-permute-start.1 = (bf16[8,24,2,1536]{3,2,1,0:T(2,128)(2,1)}, bf16[8,24,2,1536]{3,2,1,0:T(2,128)(2,1)S(1)}, u32[]{:S(2)}, u32[]{:S(2)}) collective-permute-start(bf16[8,24,2,1536]{3,2,1,0:T(2,128)(2,1)} %get-tuple-element.41), channel_id=1, source_target_pairs={{0,16},{8,24},{16,0},{24,8},{1,17},{9,25},{17,1},{25,9},{2,18},{10... | collective-permute-start | bytes 3538952 | tf_op jit(solution)/shard_map/ppermute | solution.py:194
  9.6 52.8 %collective-permute-start.2 = (bf16[8,24,2,1536]{3,2,1,0:T(2,128)(2,1)}, bf16[8,24,2,1536]{3,2,1,0:T(2,128)(2,1)S(1)}, u32[]{:S(2)}, u32[]{:S(2)}) collective-permute-start(bf16[8,24,2,1536]{3,2,1,0:T(2,128)(2,1)} %get-tuple-element.42), channel_id=1, source_target_pairs={{0,24},{8,16},{16,8},{24,0},{1,25},{9,17},{17,9},{25,1},{2,26},{10... | collective-permute-start | bytes 3538952 | tf_op jit(solution)/shard_map/ppermute | solution.py:194
  13.3 72.5 %collective-permute-start.3 = (bf16[8,24,2,1536]{3,2,1,0:T(2,128)(2,1)}, bf16[8,24,2,1536]{3,2,1,0:T(2,128)(2,1)}, u32[]{:S(2)}, u32[]{:S(2)}) collective-permute-start(bf16[8,24,2,1536]{3,2,1,0:T(2,128)(2,1)} %get-tuple-element.44), channel_id=1, source_target_pairs={{0,8},{8,0},{16,24},{24,16},{1,9},{9,1},{17,25},{25,17},{2,10},{10... | collective-permute-start | bytes 3538952 | tf_op jit(solution)/shard_map/ppermute | solution.py:194
  15.4 97.7 %collective-permute-start.4 = (bf16[8,24,2,1536]{3,2,1,0:T(2,128)(2,1)}, bf16[8,24,2,1536]{3,2,1,0:T(2,128)(2,1)}, u32[]{:S(2)}, u32[]{:S(2)}) collective-permute-start(bf16[8,24,2,1536]{3,2,1,0:T(2,128)(2,1)} %get-tuple-element.45), channel_id=1, source_target_pairs={{0,16},{8,24},{16,0},{24,8},{1,17},{9,25},{17,1},{25,9},{2,18},{10... | collective-permute-start | bytes 3538952 | tf_op jit(solution)/shard_map/ppermute | solution.py:194
  35.1 57.5 %copy-start.4 = (bf16[8,24,2,1536]{3,2,1,0:T(2,128)(2,1)}, bf16[8,24,2,1536]{3,2,1,0:T(2,128)(2,1)S(1)}, u32[]{:S(2)}) copy-start(bf16[8,24,2,1536]{3,2,1,0:T(2,128)(2,1)S(1)} %collective-permute-done.refs_0_) | copy-start | bytes 3538948
  35.1 79.5 %collective-permute-start.5 = (bf16[8,24,2,1536]{3,2,1,0:T(2,128)(2,1)}, bf16[8,24,2,1536]{3,2,1,0:T(2,128)(2,1)}, u32[]{:S(2)}, u32[]{:S(2)}) collective-permute-start(bf16[8,24,2,1536]{3,2,1,0:T(2,128)(2,1)} %get-tuple-element.46), channel_id=1, source_target_pairs={{0,24},{8,16},{16,8},{24,0},{1,25},{9,17},{17,9},{25,1},{2,26},{10... | collective-permute-start | bytes 3538952 | tf_op jit(solution)/shard_map/ppermute | solution.py:194
  62.4 30.2 %copy-start.5 = (bf16[8,24,2,1536]{3,2,1,0:T(2,128)(2,1)}, bf16[8,24,2,1536]{3,2,1,0:T(2,128)(2,1)S(1)}, u32[]{:S(2)}) copy-start(bf16[8,24,2,1536]{3,2,1,0:T(2,128)(2,1)S(1)} %collective-permute-done.1.refs_1_) | copy-start | bytes 3538948
  62.4 74.0 %collective-permute-start.6 = (bf16[8,24,2,1536]{3,2,1,0:T(2,128)(2,1)}, bf16[8,24,2,1536]{3,2,1,0:T(2,128)(2,1)}, u32[]{:S(2)}, u32[]{:S(2)}) collective-permute-start(bf16[8,24,2,1536]{3,2,1,0:T(2,128)(2,1)} %get-tuple-element.48), channel_id=1, source_target_pairs={{0,8},{8,0},{16,24},{24,16},{1,9},{9,1},{17,25},{25,17},{2,10},{10... | collective-permute-start | bytes 3538952 | tf_op jit(solution)/shard_map/ppermute | solution.py:194
  62.4 30.2 %copy-start.6 = (bf16[8,24,2,1536]{3,2,1,0:T(2,128)(2,1)}, bf16[8,24,2,1536]{3,2,1,0:T(2,128)(2,1)S(1)}, u32[]{:S(2)}) copy-start(bf16[8,24,2,1536]{3,2,1,0:T(2,128)(2,1)S(1)} %collective-permute-done.2.refs_2_) | copy-start | bytes 3538948
  62.4 126.5 %collective-permute-start.7 = (bf16[8,24,2,1536]{3,2,1,0:T(2,128)(2,1)}, bf16[8,24,2,1536]{3,2,1,0:T(2,128)(2,1)}, u32[]{:S(2)}, u32[]{:S(2)}) collective-permute-start(bf16[8,24,2,1536]{3,2,1,0:T(2,128)(2,1)} %get-tuple-element.49), channel_id=1, source_target_pairs={{0,16},{8,24},{16,0},{24,8},{1,17},{9,25},{17,1},{25,9},{2,18},{10... | collective-permute-start | bytes 3538952 | tf_op jit(solution)/shard_map/ppermute | solution.py:194
  85.8 103.1 %collective-permute-start.8 = (bf16[8,24,2,1536]{3,2,1,0:T(2,128)(2,1)}, bf16[8,24,2,1536]{3,2,1,0:T(2,128)(2,1)}, u32[]{:S(2)}, u32[]{:S(2)}) collective-permute-start(bf16[8,24,2,1536]{3,2,1,0:T(2,128)(2,1)} %get-tuple-element.50), channel_id=1, source_target_pairs={{0,24},{8,16},{16,8},{24,0},{1,25},{9,17},{17,9},{25,1},{2,26},{10... | collective-permute-start | bytes 3538952 | tf_op jit(solution)/shard_map/ppermute | solution.py:194
  113.0 99.6 %collective-permute-start.10 = (bf16[8,24,2,1536]{3,2,1,0:T(2,128)(2,1)}, bf16[8,24,2,1536]{3,2,1,0:T(2,128)(2,1)S(1)}, u32[]{:S(2)}, u32[]{:S(2)}) collective-permute-start(bf16[8,24,2,1536]{3,2,1,0:T(2,128)(2,1)} %get-tuple-element.53), channel_id=1, source_target_pairs={{0,16},{8,24},{16,0},{24,8},{1,17},{9,25},{17,1},{25,9},{2,18},{10... | collective-permute-start | bytes 3538952 | tf_op jit(solution)/shard_map/ppermute | solution.py:194
  114.6 98.1 %collective-permute-start.11 = (bf16[8,24,2,1536]{3,2,1,0:T(2,128)(2,1)}, bf16[8,24,2,1536]{3,2,1,0:T(2,128)(2,1)S(1)}, u32[]{:S(2)}, u32[]{:S(2)}) collective-permute-start(bf16[8,24,2,1536]{3,2,1,0:T(2,128)(2,1)} %get-tuple-element.54), channel_id=1, source_target_pairs={{0,24},{8,16},{16,8},{24,0},{1,25},{9,17},{17,9},{25,1},{2,26},{10... | collective-permute-start | bytes 3538952 | tf_op jit(solution)/shard_map/ppermute | solution.py:194
  136.4 76.3 %collective-permute-start.9 = (bf16[8,24,2,1536]{3,2,1,0:T(2,128)(2,1)}, bf16[8,24,2,1536]{3,2,1,0:T(2,128)(2,1)S(1)}, u32[]{:S(2)}, u32[]{:S(2)}) collective-permute-start(bf16[8,24,2,1536]{3,2,1,0:T(2,128)(2,1)} %get-tuple-element.52), channel_id=1, source_target_pairs={{0,8},{8,0},{16,24},{24,16},{1,9},{9,1},{17,25},{25,17},{2,10},{10... | collective-permute-start | bytes 3538952 | tf_op jit(solution)/shard_map/ppermute | solution.py:194
  195.8 26.1 %copy-start.14 = (f32[2,1536]{1,0:T(2,128)S(1)}, f32[2,1536]{1,0:T(2,128)}, u32[]{:S(2)}) copy-start(f32[2,1536]{1,0:T(2,128)} %get-tuple-element.43) | copy-start | bytes 36868
  212.7 1.0 copy-start.7
  212.7 1.4 copy-start.8
  214.1 1.0 copy-start.11
  235.9 33.8 %copy-start.12 = (bf16[8,24,2,1536]{3,2,1,0:T(2,128)(2,1)S(1)}, bf16[8,24,2,1536]{3,2,1,0:T(2,128)(2,1)}, u32[]{:S(2)}) copy-start(bf16[8,24,2,1536]{3,2,1,0:T(2,128)(2,1)} %get-tuple-element.58) | copy-start | bytes 3538948
  269.7 32.6 %copy-start.13 = (bf16[8,24,2,1536]{3,2,1,0:T(2,128)(2,1)S(1)}, bf16[8,24,2,1536]{3,2,1,0:T(2,128)(2,1)}, u32[]{:S(2)}) copy-start(bf16[8,24,2,1536]{3,2,1,0:T(2,128)(2,1)} %get-tuple-element.57) | copy-start | bytes 3538948
  334.8 32.9 %all-to-all-start.1 = ((bf16[8,24,2,1536]{3,2,1,0:T(2,128)(2,1)}), bf16[8,24,2,1536]{3,2,1,0:T(2,128)(2,1)S(1)}, u32[]{:S(2)}, u32[]{:S(2)}) async-start(bf16[8,24,2,1536]{3,2,1,0:T(2,128)(2,1)} %get-tuple-element.56), calls=%async_computation.1 | async-start | bytes 2359296 | tf_op jit(solution)/shard_map/all_to_all | solution.py:197
  367.6 1.0 copy-start.3
  368.7 32.9 %all-to-all-start.8 = ((bf16[8,24,2,1536]{3,2,1,0:T(2,128)(2,1)}), bf16[8,24,2,1536]{3,2,1,0:T(2,128)(2,1)S(1)}, u32[]{:S(2)}, u32[]{:S(2)}) async-start(bf16[8,24,2,1536]{3,2,1,0:T(2,128)(2,1)} %get-tuple-element.75), calls=%async_computation.8 | async-start | bytes 2359296 | tf_op jit(solution)/shard_map/all_to_all | solution.py:197
  401.5 70.7 %copy-start = (bf16[8,24,2,1536]{3,2,1,0:T(2,128)(2,1)}, bf16[8,24,2,1536]{3,2,1,0:T(2,128)(2,1)S(1)}, u32[]{:S(2)}) copy-start(bf16[8,24,2,1536]{3,2,1,0:T(2,128)(2,1)S(1)} %all-to-all-done.8.refs_0_) | copy-start | bytes 3538948
  401.5 32.9 %all-to-all-start.7 = ((bf16[8,24,2,1536]{3,2,1,0:T(2,128)(2,1)}), bf16[8,24,2,1536]{3,2,1,0:T(2,128)(2,1)S(1)}, u32[]{:S(2)}, u32[]{:S(2)}) async-start(bf16[8,24,2,1536]{3,2,1,0:T(2,128)(2,1)} %get-tuple-element.74), calls=%async_computation.7 | async-start | bytes 2359296 | tf_op jit(solution)/shard_map/all_to_all | solution.py:197
  434.4 39.8 %copy-start.1 = (bf16[8,24,2,1536]{3,2,1,0:T(2,128)(2,1)}, bf16[8,24,2,1536]{3,2,1,0:T(2,128)(2,1)S(1)}, u32[]{:S(2)}) copy-start(bf16[8,24,2,1536]{3,2,1,0:T(2,128)(2,1)S(1)} %all-to-all-done.7.refs_0_) | copy-start | bytes 3538948
  434.4 32.9 %all-to-all-start.6 = ((bf16[8,24,2,1536]{3,2,1,0:T(2,128)(2,1)}), bf16[8,24,2,1536]{3,2,1,0:T(2,128)(2,1)S(1)}, u32[]{:S(2)}, u32[]{:S(2)}) async-start(bf16[8,24,2,1536]{3,2,1,0:T(2,128)(2,1)} %get-tuple-element.73), calls=%async_computation.6 | async-start | bytes 2359296 | tf_op jit(solution)/shard_map/all_to_all | solution.py:197
  467.3 60.6 %copy-start.2 = (bf16[8,24,2,1536]{3,2,1,0:T(2,128)(2,1)}, bf16[8,24,2,1536]{3,2,1,0:T(2,128)(2,1)S(1)}, u32[]{:S(2)}) copy-start(bf16[8,24,2,1536]{3,2,1,0:T(2,128)(2,1)S(1)} %all-to-all-done.6.refs_0_) | copy-start | bytes 3538948
  467.3 33.6 %all-to-all-start.5 = ((bf16[8,24,2,1536]{3,2,1,0:T(2,128)(2,1)}), bf16[8,24,2,1536]{3,2,1,0:T(2,128)(2,1)}, u32[]{:S(2)}, u32[]{:S(2)}) async-start(bf16[8,24,2,1536]{3,2,1,0:T(2,128)(2,1)} %get-tuple-element.72), calls=%async_computation.5 | async-start | bytes 2359296 | tf_op jit(solution)/shard_map/all_to_all | solution.py:197
  471.5 29.4 %collective-permute-start.21 = (bf16[8,24,2,1536]{3,2,1,0:T(2,128)(2,1)S(1)}, bf16[8,24,2,1536]{3,2,1,0:T(2,128)(2,1)}, u32[]{:S(2)}, u32[]{:S(2)}) collective-permute-start(bf16[8,24,2,1536]{3,2,1,0:T(2,128)(2,1)S(1)} %all-to-all-done.8.refs_0_), channel_id=1, source_target_pairs={{0,8},{8,0},{16,24},{24,16},{1,9},{9,1},{17,25},{25,17},{2,10},{10... | collective-permute-start | bytes 3538952 | tf_op jit(solution)/shard_map/ppermute | solution.py:194
  472.2 29.3 %collective-permute-start.23 = (bf16[8,24,2,1536]{3,2,1,0:T(2,128)(2,1)S(1)}, bf16[8,24,2,1536]{3,2,1,0:T(2,128)(2,1)}, u32[]{:S(2)}, u32[]{:S(2)}) collective-permute-start(bf16[8,24,2,1536]{3,2,1,0:T(2,128)(2,1)S(1)} %all-to-all-done.8.refs_0_), channel_id=1, source_target_pairs={{0,16},{8,24},{16,0},{24,8},{1,17},{9,25},{17,1},{25,9},{2,18},{10... | collective-permute-start | bytes 3538952 | tf_op jit(solution)/shard_map/ppermute | solution.py:194
  472.8 53.6 %collective-permute-start.18 = (bf16[8,24,2,1536]{3,2,1,0:T(2,128)(2,1)S(1)}, bf16[8,24,2,1536]{3,2,1,0:T(2,128)(2,1)}, u32[]{:S(2)}, u32[]{:S(2)}) collective-permute-start(bf16[8,24,2,1536]{3,2,1,0:T(2,128)(2,1)S(1)} %all-to-all-done.7.refs_0_), channel_id=1, source_target_pairs={{0,16},{8,24},{16,0},{24,8},{1,17},{9,25},{17,1},{25,9},{2,18},{10... | collective-permute-start | bytes 3538952 | tf_op jit(solution)/shard_map/ppermute | solution.py:194
  474.2 53.6 %collective-permute-start.20 = (bf16[8,24,2,1536]{3,2,1,0:T(2,128)(2,1)S(1)}, bf16[8,24,2,1536]{3,2,1,0:T(2,128)(2,1)}, u32[]{:S(2)}, u32[]{:S(2)}) collective-permute-start(bf16[8,24,2,1536]{3,2,1,0:T(2,128)(2,1)S(1)} %all-to-all-done.7.refs_0_), channel_id=1, source_target_pairs={{0,8},{8,0},{16,24},{24,16},{1,9},{9,1},{17,25},{25,17},{2,10},{10... | collective-permute-start | bytes 3538952 | tf_op jit(solution)/shard_map/ppermute | solution.py:194
  475.7 75.4 %collective-permute-start.15 = (bf16[8,24,2,1536]{3,2,1,0:T(2,128)(2,1)S(1)}, bf16[8,24,2,1536]{3,2,1,0:T(2,128)(2,1)}, u32[]{:S(2)}, u32[]{:S(2)}) collective-permute-start(bf16[8,24,2,1536]{3,2,1,0:T(2,128)(2,1)S(1)} %all-to-all-done.6.refs_0_), channel_id=1, source_target_pairs={{0,8},{8,0},{16,24},{24,16},{1,9},{9,1},{17,25},{25,17},{2,10},{10... | collective-permute-start | bytes 3538952 | tf_op jit(solution)/shard_map/ppermute | solution.py:194
  500.9 50.8 %collective-permute-start.12 = (bf16[8,24,2,1536]{3,2,1,0:T(2,128)(2,1)}, bf16[8,24,2,1536]{3,2,1,0:T(2,128)(2,1)}, u32[]{:S(2)}, u32[]{:S(2)}) collective-permute-start(bf16[8,24,2,1536]{3,2,1,0:T(2,128)(2,1)} %all-to-all-done.5.refs_0_), channel_id=1, source_target_pairs={{0,16},{8,24},{16,0},{24,8},{1,17},{9,25},{17,1},{25,9},{2,18},{10... | collective-permute-start | bytes 3538952 | tf_op jit(solution)/shard_map/ppermute | solution.py:194
  501.5 75.5 %collective-permute-start.22 = (bf16[8,24,2,1536]{3,2,1,0:T(2,128)(2,1)}, bf16[8,24,2,1536]{3,2,1,0:T(2,128)(2,1)}, u32[]{:S(2)}, u32[]{:S(2)}) collective-permute-start(bf16[8,24,2,1536]{3,2,1,0:T(2,128)(2,1)} %collective-permute-done.21.refs_1_), channel_id=1, source_target_pairs={{0,16},{8,24},{16,0},{24,8},{1,17},{9,25},{17,1},{25,9},{2,18},{10... | collective-permute-start | bytes 3538952 | tf_op jit(solution)/shard_map/ppermute | solution.py:194
  526.4 62.5 %collective-permute-start.19 = (bf16[8,24,2,1536]{3,2,1,0:T(2,128)(2,1)}, bf16[8,24,2,1536]{3,2,1,0:T(2,128)(2,1)}, u32[]{:S(2)}, u32[]{:S(2)}) collective-permute-start(bf16[8,24,2,1536]{3,2,1,0:T(2,128)(2,1)} %collective-permute-done.18.refs_2_), channel_id=1, source_target_pairs={{0,8},{8,0},{16,24},{24,16},{1,9},{9,1},{17,25},{25,17},{2,10},{10... | collective-permute-start | bytes 3538952 | tf_op jit(solution)/shard_map/ppermute | solution.py:194
  527.9 74.3 %collective-permute-start.17 = (bf16[8,24,2,1536]{3,2,1,0:T(2,128)(2,1)S(1)}, bf16[8,24,2,1536]{3,2,1,0:T(2,128)(2,1)S(1)}, u32[]{:S(2)}, u32[]{:S(2)}) collective-permute-start(bf16[8,24,2,1536]{3,2,1,0:T(2,128)(2,1)S(1)} %all-to-all-done.6.refs_0_), channel_id=1, source_target_pairs={{0,16},{8,24},{16,0},{24,8},{1,17},{9,25},{17,1},{25,9},{2,18},{10... | collective-permute-start | bytes 3538952 | tf_op jit(solution)/shard_map/ppermute | solution.py:194
  551.1 75.5 %collective-permute-start.16 = (bf16[8,24,2,1536]{3,2,1,0:T(2,128)(2,1)}, bf16[8,24,2,1536]{3,2,1,0:T(2,128)(2,1)}, u32[]{:S(2)}, u32[]{:S(2)}) collective-permute-start(bf16[8,24,2,1536]{3,2,1,0:T(2,128)(2,1)} %collective-permute-done.15.refs_1_), channel_id=1, source_target_pairs={{0,16},{8,24},{16,0},{24,8},{1,17},{9,25},{17,1},{25,9},{2,18},{10... | collective-permute-start | bytes 3538952 | tf_op jit(solution)/shard_map/ppermute | solution.py:194
  551.7 77.2 %collective-permute-start.14 = (bf16[8,24,2,1536]{3,2,1,0:T(2,128)(2,1)}, bf16[8,24,2,1536]{3,2,1,0:T(2,128)(2,1)}, u32[]{:S(2)}, u32[]{:S(2)}) collective-permute-start(bf16[8,24,2,1536]{3,2,1,0:T(2,128)(2,1)} %all-to-all-done.5.refs_0_), channel_id=1, source_target_pairs={{0,8},{8,0},{16,24},{24,16},{1,9},{9,1},{17,25},{25,17},{2,10},{10... | collective-permute-start | bytes 3538952 | tf_op jit(solution)/shard_map/ppermute | solution.py:194
  577.0 55.7 %collective-permute-start.13 = (bf16[8,24,2,1536]{3,2,1,0:T(2,128)(2,1)}, bf16[8,24,2,1536]{3,2,1,0:T(2,128)(2,1)S(1)}, u32[]{:S(2)}, u32[]{:S(2)}) collective-permute-start(bf16[8,24,2,1536]{3,2,1,0:T(2,128)(2,1)} %collective-permute-done.12.refs_2_), channel_id=1, source_target_pairs={{0,8},{8,0},{16,24},{24,16},{1,9},{9,1},{17,25},{25,17},{2,10},{10... | collective-permute-start | bytes 3538952 | tf_op jit(solution)/shard_map/ppermute | solution.py:194
  602.1 1.0 copy-start.10
  632.7 1.1 copy-start.9
